TPU v7x, 32 devices: a whole 2x2x4 slice. The times are simulated.
32 devices in a mesh: dp: 16 (over z, x, core), rep: 2 (over y).
Axes of the slice: x: 2, y: 2, z: 4, core: 2. Of those that a mesh axis runs over, the one named last changes fastest.
Arguments:
- tokens: bfloat16 [48, 261, 768], P('dp'), may hold values from -6 to 6
- text_len: int32 [48], P('dp'), may hold values from 1 to 64, as said below
- routes: int32 [48, 261], P('dp'), may hold values from 0 to 2, as said below
- attn_gain: float32 [768], replicated, may hold values from 0.5 to 1.5
- attn_shift: float32 [768], replicated, may hold values from -1 to 1
- w_qkv: bfloat16 [3, 768, 768], P(None, 'dp', 'rep'), may hold values from -0.21875 to 0.21875
- b_qv: float32 [2, 768], P(None, 'rep'), may hold values from -1.5 to 1.5
- w_out: bfloat16 [768, 768], P('dp', 'rep'), may hold values from -1.25 to 1.25
- b_out: float32 [768], replicated, may hold values from -0.5 to 0.5
- ffn_gain: float32 [768], replicated, may hold values from 0.5 to 1.5
- ffn_shift: float32 [768], replicated, may hold values from -1 to 1
- w_up: bfloat16 [3, 768, 3072], P(None, 'dp', 'rep'), may hold values from -0.21875 to 0.21875
- b_up: float32 [3, 3072], P(None, 'rep'), may hold values from -1.5 to 1.5
- w_down: bfloat16 [3, 768, 3072], P(None, 'dp', 'rep'), may hold values from -0.15625 to 0.15625
- b_down: float32 [3, 768], replicated, may hold values from -0.5 to 0.5
- cotangent: bfloat16 [48, 261, 768], P('dp'), may hold values from -6 to 6
Outputs:
- output: bfloat16 [48, 261, 768], P('dp')
- grad_tokens: float32 [48, 261, 768], P('dp')
- grad_w_qkv: float32 [3, 768, 768], P(None, 'dp', 'rep')
- grad_w_out: float32 [768, 768], P('dp', 'rep')
- grad_w_up: float32 [3, 768, 3072], P(None, 'dp', 'rep')
- grad_w_down: float32 [3, 768, 3072], P(None, 'dp', 'rep')
- grad_b_qv: float32 [2, 768], P(None, 'rep')
- grad_b_out: float32 [768], replicated
- grad_b_up: float32 [3, 3072], P(None, 'rep')
- grad_b_down: float32 [3, 768], replicated
- grad_norms: float32 [4, 768], replicated
Inputs may be any that keep to these rules, and one draw needn't show every extreme that they name: `text_len`: text rows in use of each item; some item uses all 64 in every draw. `routes`: routing by modality: each item either sends its first 197 rows to expert 0 and its other rows to expert 1, or sends all its rows to expert 2; both kinds of item occur in every draw.
All inputs are finite; a program needn't handle non-finite values.
Results may differ from a plain program's by a relative error of at most 0.014.
Values may be sent and summed in bfloat16 or wider, within the bound.
No kernel may reach another device: no remote copies, remote signals or barrier semaphores. Data moves between devices by JAX's collectives and lax.ppermute only.
A program may use at most 192 MiB of HBM per device.

v0:
```python
import math
import jax
import jax.numpy as jnp
from jax import lax
from jax.sharding import PartitionSpec as P

HDIM = 64
IMG = 197
EPSILON = 1e-05
TILE = 128
ROOT_HALF = 0.7071067811865476
INV_ROOT_TAU = 0.3989422804014327
HIGHEST = lax.Precision.HIGHEST


def norm_rows(vector, gain_vec, shift_vec):
    row_mean = jnp.mean(vector, axis=-1, keepdims=True)
    centred = vector - row_mean
    row_var = jnp.mean(centred * centred, axis=-1, keepdims=True)
    spread = lax.rsqrt(row_var + EPSILON)
    normal_rows = centred * spread
    return (normal_rows * gain_vec + shift_vec, normal_rows, spread)


def norm_back(grad_rows, normal_rows, spread, gain_vec):
    scaled = grad_rows * gain_vec
    return spread * (
        scaled
        - jnp.mean(scaled, axis=-1, keepdims=True)
        - normal_rows * jnp.mean(scaled * normal_rows, axis=-1, keepdims=True)
    )


def gelu_slope(pre_act):
    return (
        0.5 * (1.0 + lax.erf(pre_act * ROOT_HALF))
        + pre_act * jnp.exp(-0.5 * pre_act * pre_act) * INV_ROOT_TAU
    )


def packing(route_flat, expert_count, row_count):
    tile_count = -(-row_count // TILE) + expert_count
    route_hits = (route_flat[:, None] == jnp.arange(expert_count, dtype=jnp.int32)[None, :]).astype(
        jnp.int32
    )
    counts = jnp.sum(route_hits, axis=0)
    padded = (counts + TILE - 1) // TILE * TILE
    group_end = jnp.cumsum(padded)
    group_start = group_end - padded
    before = jnp.cumsum(route_hits, axis=0) - route_hits
    target = jnp.sum(route_hits * (before + group_start[None, :]), axis=1)
    tile_start = jnp.arange(tile_count, dtype=jnp.int32) * TILE
    tile_owner = jnp.minimum(
        jnp.sum((tile_start[:, None] >= group_end[None, :]).astype(jnp.int32), axis=1),
        expert_count - 1,
    )
    return (target, tile_owner, tile_count)


def per_device(
    tokens,
    text_len,
    routes,
    attn_gain,
    attn_shift,
    w_qkv,
    b_qv,
    w_out,
    b_out,
    ffn_gain,
    ffn_shift,
    w_up,
    b_up,
    w_down,
    b_down,
    cotangent,
):
    item_count, seq_len, model_width = tokens.shape
    row_count = item_count * seq_len
    local_width = w_qkv.shape[2]
    local_heads = local_width // HDIM
    expert_count = w_up.shape[0]
    score_scale = 1.0 / math.sqrt(HDIM)
    contract_last = (((1,), (1,)), ((), ()))
    contract_first = (((0,), (0,)), ((), ()))
    inputs = tokens.reshape(row_count, model_width).astype(jnp.float32)
    first_normed, first_hat, first_spread = norm_rows(inputs, attn_gain, attn_shift)
    first_low = first_normed.astype(jnp.bfloat16)
    qkv_full, out_full = (
        lax.all_gather(w_qkv, "dp", axis=1, tiled=True),
        lax.all_gather(w_out, "dp", axis=0, tiled=True),
    )
    projected = jnp.einsum("rd,tde->tre", first_low, qkv_full, preferred_element_type=jnp.float32)
    bias_rows = jnp.stack([b_qv[0], jnp.zeros_like(b_qv[0]), b_qv[1]])
    proj_low = (projected + bias_rows[:, None, :]).astype(jnp.bfloat16)
    head_split = proj_low.reshape(3, item_count, seq_len, local_heads, HDIM)
    queries, key_rows, values = (head_split[0], head_split[1], head_split[2])
    key_ok = jnp.arange(seq_len, dtype=jnp.int32)[None, :] < (IMG + text_len)[:, None]

    def scores_of(query_part, key_part):
        raw_scores = (
            jnp.einsum("ishd,ijhd->ihsj", query_part, key_part, preferred_element_type=jnp.float32)
            * score_scale
        )
        return jnp.where(key_ok[:, None, None, :], raw_scores, -1e30)

    raw_scores = scores_of(queries, key_rows)
    row_max = jnp.max(raw_scores, axis=-1, keepdims=True)
    raised = jnp.exp(raw_scores - row_max)
    row_total = jnp.sum(raised, axis=-1, keepdims=True)
    attn_probs = raised / row_total
    log_total = row_max + jnp.log(row_total)
    probs_low = attn_probs.astype(jnp.bfloat16)
    context = jnp.einsum("ihsj,ijhd->ishd", probs_low, values, preferred_element_type=jnp.float32)
    context_low = context.reshape(row_count, local_width).astype(jnp.bfloat16)
    attn_part = lax.dot_general(
        context_low, out_full, contract_last, preferred_element_type=jnp.float32
    )
    attn_share = lax.psum_scatter(
        attn_part.astype(jnp.bfloat16), "rep", scatter_dimension=1, tiled=True
    ).astype(jnp.float32)
    attn_sum = lax.all_gather(attn_share.astype(jnp.bfloat16), "rep", axis=1, tiled=True).astype(
        attn_share.dtype
    )
    residual = inputs + (attn_sum + b_out)
    second_normed, second_hat, second_spread = norm_rows(residual, ffn_gain, ffn_shift)
    second_low = second_normed.astype(jnp.bfloat16)
    route_flat = routes.reshape(row_count)
    target, tile_owner, tile_count = packing(route_flat, expert_count, row_count)
    packed_input = (
        jnp.zeros((tile_count * TILE, model_width), jnp.bfloat16)
        .at[target]
        .set(second_low)
        .reshape(tile_count, TILE, model_width)
    )
    up_full, down_full = (
        lax.all_gather(w_up, "dp", axis=1, tiled=True),
        lax.all_gather(w_down, "dp", axis=1, tiled=True),
    )
    owner_hot = (tile_owner[:, None] == jnp.arange(expert_count, dtype=jnp.int32)[None, :]).astype(
        jnp.float32
    )
    up_projection_tiles = up_full[tile_owner]
    down_projection_tiles = down_full[tile_owner]
    pre_acts = (
        jnp.einsum(
            "pim,pmj->pij", packed_input, up_projection_tiles, preferred_element_type=jnp.float32
        )
        + jnp.dot(owner_hot, b_up, precision=HIGHEST)[:, None, :]
    )
    activated_rows = jax.nn.gelu(pre_acts, approximate=False).astype(jnp.bfloat16)
    partial_sums = jnp.einsum(
        "wmy,wny->wmn", activated_rows, down_projection_tiles, preferred_element_type=jnp.float32
    )
    ffn_rows = partial_sums.reshape(tile_count * TILE, model_width)[target]
    ffn_share = lax.psum_scatter(
        ffn_rows.astype(jnp.bfloat16), "rep", scatter_dimension=1, tiled=True
    ).astype(jnp.float32)
    ffn_sum = lax.all_gather(ffn_share.astype(jnp.bfloat16), "rep", axis=1, tiled=True).astype(
        ffn_share.dtype
    )
    route_pick = (route_flat[:, None] == jnp.arange(expert_count, dtype=jnp.int32)[None, :]).astype(
        jnp.float32
    )
    output = residual + (ffn_sum + jnp.dot(route_pick, b_down, precision=HIGHEST))
    output_low = output.astype(jnp.bfloat16).reshape(item_count, seq_len, model_width)
    grad_low = cotangent.reshape(row_count, model_width)
    grad_out = grad_low.astype(jnp.float32)
    grad_b_down = jnp.dot(route_pick.T, grad_out, precision=HIGHEST)
    up_back, down_back, qkv_back, out_back = (
        lax.all_gather(w_up, "dp", axis=1, tiled=True),
        lax.all_gather(w_down, "dp", axis=1, tiled=True),
        lax.all_gather(w_qkv, "dp", axis=1, tiled=True),
        lax.all_gather(w_out, "dp", axis=0, tiled=True),
    )
    up_gradient_tiles = up_back[tile_owner]
    down_gradient_tiles = down_back[tile_owner]
    packed_gradient = (
        jnp.zeros((tile_count * TILE, model_width), jnp.bfloat16)
        .at[target]
        .set(grad_low)
        .reshape(tile_count, TILE, model_width)
    )
    grad_active = jnp.einsum(
        "pim,pmj->pij", packed_gradient, down_gradient_tiles, preferred_element_type=jnp.float32
    )
    gradient_before_activation = (grad_active * gelu_slope(pre_acts)).astype(jnp.bfloat16)
    grad_tiles = jnp.einsum(
        "wmy,wny->wmn",
        gradient_before_activation,
        up_gradient_tiles,
        preferred_element_type=jnp.float32,
    )
    down_terms = jnp.einsum(
        "jxa,jxm->jam", packed_gradient, activated_rows, preferred_element_type=jnp.float32
    )
    grad_down_local = jnp.einsum("te,tdf->edf", owner_hot, down_terms, precision=HIGHEST)
    up_projection_terms = jnp.einsum(
        "jxa,jxm->jam", packed_input, gradient_before_activation, preferred_element_type=jnp.float32
    )
    grad_up_local = jnp.einsum("te,tdf->edf", owner_hot, up_projection_terms, precision=HIGHEST)
    grad_b_up = jnp.dot(
        owner_hot.T,
        jnp.sum(gradient_before_activation.astype(jnp.float32), axis=1),
        precision=HIGHEST,
    )
    back_rows = grad_tiles.reshape(tile_count * TILE, model_width)[target]
    second_share = lax.psum_scatter(
        back_rows.astype(jnp.bfloat16), "rep", scatter_dimension=1, tiled=True
    ).astype(jnp.float32)
    grad_second = lax.all_gather(
        second_share.astype(jnp.bfloat16), "rep", axis=1, tiled=True
    ).astype(second_share.dtype)
    grad_ffn_gain = jnp.sum(grad_second * second_hat, axis=0)
    grad_ffn_shift = jnp.sum(grad_second, axis=0)
    grad_residual = grad_out + norm_back(grad_second, second_hat, second_spread, ffn_gain)
    grad_w_up, grad_w_down = (
        lax.psum_scatter(grad_up_local, "dp", scatter_dimension=1, tiled=True),
        lax.psum_scatter(grad_down_local, "dp", scatter_dimension=1, tiled=True),
    )
    grad_branch = grad_residual.astype(jnp.bfloat16)
    grad_b_out = jnp.sum(grad_branch.astype(jnp.float32), axis=0)
    grad_context = jnp.dot(grad_branch, out_back, preferred_element_type=jnp.float32)
    grad_ctx_low = grad_context.astype(jnp.bfloat16).reshape(item_count, seq_len, local_heads, HDIM)
    grad_out_local = lax.dot_general(
        grad_branch, context_low, contract_first, preferred_element_type=jnp.float32
    )
    again_scores = scores_of(queries, key_rows)
    again_probs = jnp.exp(again_scores - log_total)
    again_low = again_probs.astype(jnp.bfloat16)
    grad_probs = jnp.einsum(
        "ishd,ijhd->ihsj", grad_ctx_low, values, preferred_element_type=jnp.float32
    )
    grad_values = jnp.einsum(
        "ihsj,ishd->ijhd", again_low, grad_ctx_low, preferred_element_type=jnp.float32
    )
    inner_sum = jnp.sum(again_probs * grad_probs, axis=-1, keepdims=True)
    grad_scores = (again_probs * (grad_probs - inner_sum)).astype(jnp.bfloat16)
    grad_queries = (
        jnp.einsum("ihsj,ijhd->ishd", grad_scores, key_rows, preferred_element_type=jnp.float32)
        * score_scale
    )
    grad_keys = (
        jnp.einsum("ihsj,ishd->ijhd", grad_scores, queries, preferred_element_type=jnp.float32)
        * score_scale
    )
    grad_proj = (
        jnp.stack([grad_queries, grad_keys, grad_values])
        .reshape(3, row_count, local_width)
        .astype(jnp.bfloat16)
    )
    grad_b_qv = jnp.stack(
        [
            jnp.sum(grad_proj[0].astype(jnp.float32), axis=0),
            jnp.sum(grad_proj[2].astype(jnp.float32), axis=0),
        ]
    )
    grad_qkv_local = jnp.einsum(
        "rd,tre->tde", first_low, grad_proj, preferred_element_type=jnp.float32
    )
    back_first = jnp.einsum("tre,tde->rd", grad_proj, qkv_back, preferred_element_type=jnp.float32)
    first_share = lax.psum_scatter(
        back_first.astype(jnp.bfloat16), "rep", scatter_dimension=1, tiled=True
    ).astype(jnp.float32)
    grad_first = lax.all_gather(first_share.astype(jnp.bfloat16), "rep", axis=1, tiled=True).astype(
        first_share.dtype
    )
    grad_attn_gain = jnp.sum(grad_first * first_hat, axis=0)
    grad_attn_shift = jnp.sum(grad_first, axis=0)
    grad_inputs = grad_residual + norm_back(grad_first, first_hat, first_spread, attn_gain)
    grad_w_qkv, grad_w_out = (
        lax.psum_scatter(grad_qkv_local, "dp", scatter_dimension=1, tiled=True),
        lax.psum_scatter(grad_out_local, "dp", scatter_dimension=0, tiled=True),
    )
    norm_local = jnp.stack([grad_attn_gain, grad_attn_shift, grad_ffn_gain, grad_ffn_shift])
    total_qv, total_out, total_up, total_down, total_norms = lax.psum(
        (grad_b_qv, grad_b_out, grad_b_up, grad_b_down, norm_local), "dp"
    )
    return (
        output_low,
        grad_inputs.reshape(item_count, seq_len, model_width),
        grad_w_qkv,
        grad_w_out,
        grad_w_up,
        grad_w_down,
        total_qv,
        total_out,
        total_up,
        total_down,
        total_norms,
    )


def solution(mesh):
    return jax.shard_map(
        per_device,
        mesh=mesh,
        in_specs=(
            P("dp", None, None),
            P("dp"),
            P("dp", None),
            P(),
            P(),
            P(None, "dp", "rep"),
            P(None, "rep"),
            P("dp", "rep"),
            P(),
            P(),
            P(),
            P(None, "dp", "rep"),
            P(None, "rep"),
            P(None, "dp", "rep"),
            P(),
            P("dp", None, None),
        ),
        out_specs=(
            P("dp", None, None),
            P("dp", None, None),
            P(None, "dp", "rep"),
            P("dp", "rep"),
            P(None, "dp", "rep"),
            P(None, "dp", "rep"),
            P(None, "rep"),
            P(),
            P(None, "rep"),
            P(),
            P(),
        ),
        check_vma=False,
    )
```

profile of v0, /device:TPU:0, one launch (start us, length us, event | category | flops | bytes accessed | tf_op | source)
XLA Modules:
  0.0 1421.6 jit_solution(17374396237260171322)
XLA Ops:
  14.2 27.1 %all_gather.29 = bf16[768,384]{1,0:T(8,128)(2,1)} all-gather(bf16[48,384]{1,0:T(8,128)(2,1)S(1)} %copy-done.33), channel_id=1, replica_groups=mesh['dp'=16,'rep'=2] {'dp'}, dimensions={0}, use_global_device_ids=true | all-gather | bytes 626688 | tf_op jit(solution)/shard_map/all_gather | solution.py:91
  41.3 13.2 all-gather.8.cloned.1.call-done
  54.5 3.4 fusion.44
  79.3 22.8 %reduce-scatter.16.cloned.1.call-done = bf16[384,783]{1,0:T(8,128)(2,1)} async-done(((bf16[768,783]{1,0:T(8,128)(2,1)}), bf16[384,783]{1,0:T(8,128)(2,1)}) %reduce-scatter.16.cloned.1.call-update) | async-done | bytes 601360
  109.2 7.1 scatter_custom_fusion.1
  116.8 10.7 all-gather.10.cloned.1.call-done
  130.4 7.9 scatter_custom_fusion
  138.2 57.4 %all-gather.12.cloned.1.call-done = bf16[3,768,1536]{2,1,0:T(8,128)(2,1)} async-done(((bf16[3,48,1536]{2,1,0:T(8,128)(2,1)}), bf16[3,768,1536]{2,1,0:T(8,128)(2,1)}) %all-gather.12.cloned.1.call-update) | async-done | bytes 7077904 | tf_op jit(solution)/shard_map/all_gather | solution.py:137
  195.7 6.5 fusion.96
  202.1 8.3 gather_fusion.2
  210.5 7.8 gather_fusion.3
  218.3 10.3 constant_dynamic-update-slice_fusion.1
  228.6 34.1 %all-gather.14.cloned.1.call-done = bf16[3,768,1536]{2,1,0:T(8,128)(2,1)} async-done(((bf16[3,48,1536]{2,1,0:T(8,128)(2,1)}), bf16[3,768,1536]{2,1,0:T(8,128)(2,1)}) %all-gather.14.cloned.1.call-update) | async-done | bytes 7077904 | tf_op jit(solution)/shard_map/all_gather | solution.py:138
  262.7 6.5 fusion.95
  269.2 7.8 gather_fusion.4
  277.0 10.1 constant_dynamic-update-slice_fusion.3
  287.1 7.8 gather_fusion.5
  294.9 10.6 constant_dynamic-update-slice_fusion
  307.0 5.2 constant_dynamic-update-slice_fusion.2
  312.3 14.1 fusion.22
  326.3 15.7 %convert_reduce_fusion = (f32[10,1536]{1,0:T(8,128)}, bf16[10,128,1536]{2,1,0:T(8,128)(2,1)}) fusion(f32[10,128,1536]{2,1,0:T(8,128)} %get-tuple-element.99, f32[10,1536]{1,0:T(8,128)S(1)} %fusion.73, bf16[10,128,768]{2,1,0:T(8,128)(2,1)S(1)} %bitcast.105, bf16[10,768,1536]{2,1,0:T(8,128)(2,1)} %constant_dynamic-update-slice_fusion.2), kind=kOutput, calls=%fused_computation.28 | convolution fusion | flops 3045442560 | bytes 37478400 | tf_op jit(solution)/shard_map/pim,pmj->pij/dot_general | solution.py:184
  342.0 13.8 fusion.100
  355.8 6.6 gather_fusion.1
  362.3 2.5 copy.172
  364.9 20.1 %fusion.6 = bf16[10,128,1536]{2,1,0:T(8,128)(2,1)} fusion(f32[10,128,1536]{2,1,0:T(8,128)} %get-tuple-element.99, f32[10,1536]{1,0:T(8,128)S(1)} %fusion.73, u16[128,1536]{1,0:T(8,128)(2,1)} %get-tuple-element.67, u16[128,1536]{1,0:T(8,128)(2,1)} %get-tuple-element.66), kind=kLoop, calls=%fused_computation.16 | loop fusion | flops 139591680 | bytes 12644352 | tf_op jit(solution)/shard_map/convert_element_type | solution.py:151
  385.0 13.7 fusion.99
  398.7 6.6 gather_fusion
  405.3 2.5 copy.170
  410.0 20.8 %fusion.101 = f32[10,768,1536]{2,1,0:T(8,128)} fusion(bf16[10,128,768]{2,1,0:T(8,128)(2,1)} %bitcast.103, bf16[10,128,1536]{2,1,0:T(8,128)(2,1)} %get-tuple-element.103), kind=kOutput, calls=%fused_computation.193 | convolution fusion | flops 3019898880 | bytes 53084160 | tf_op jit(solution)/shard_map/jxa,jxm->jam/dot_general | solution.py:198
  431.9 2.6 fusion.42
  440.4 5.3 fusion.50
  450.2 6.7 multiply_reduce_fusion
  457.0 2.6 multiply_convert_fusion
  465.4 3.0 fusion.53
  470.9 3.6 bitcast_convert_fusion
  476.3 67.0 %fusion.2 = f32[3,768,1536]{2,0,1:T(4,128)} fusion(f32[10,768,1536]{2,1,0:T(8,128)} %fusion.101, s32[10]{0:T(128)S(1)} %copy-done.43), kind=kOutput, calls=%fused_computation.10 | convolution fusion | flops 424673312 | bytes 61341736 | tf_op jit(solution)/shard_map/te,tdf->edf/dot_general | solution.py:201
  545.6 21.0 %fusion.102 = f32[10,768,1536]{2,1,0:T(8,128)} fusion(bf16[10,128,768]{2,1,0:T(8,128)(2,1)S(1)} %bitcast.106, bf16[10,128,1536]{2,1,0:T(8,128)(2,1)} %fusion.6), kind=kOutput, calls=%fused_computation.194 | convolution fusion | flops 3019898880 | bytes 53084160 | tf_op jit(solution)/shard_map/jxa,jxm->jam/dot_general | solution.py:194
  568.9 67.0 %fusion = f32[3,768,1536]{2,0,1:T(4,128)} fusion(f32[10,768,1536]{2,1,0:T(8,128)} %fusion.102, s32[10]{0:T(128)S(1)} %copy-done.43), kind=kOutput, calls=%fused_computation.8 | convolution fusion | flops 424673312 | bytes 61341736 | tf_op jit(solution)/shard_map/te,tdf->edf/dot_general | solution.py:197
  636.0 5.4 convolution_bitcast_fusion
  641.4 6.3 copy.153
  651.3 3.7 add_convert_fusion.1
  655.1 2.6 reshape.314
  659.3 4.0 fusion.84
  663.4 2.6 fusion.43
  668.1 3.4 reshape.319
  671.5 65.2 %all-reduce.4 = (f32[2,384]{1,0:T(2,128)}, f32[768]{0:T(1024)}, f32[3,1536]{1,0:T(4,128)}, f32[3,768]{1,0:T(4,128)}, f32[4,768]{1,0:T(4,128)}) all-reduce(f32[2,384]{1,0:T(2,128)S(1)} %pad_maximum_fusion.5, f32[768]{0:T(1024)S(1)} %get-tuple-element.84, f32[3,1536]{1,0:T(4,128)S(1)} %fusion.71, ...), channel_id=1, replica_groups=mesh['dp'=16,'rep'=2] {'dp'}, use_global_device_ids=true, to_apply=%region_29.30 | all-reduce | flops 11520 | bytes 92160 | tf_op jit(solution)/shard_map/psum | solution.py:276
  736.8 615.4 %all-reduce.8.cloned.1.call-done = (f32[3,768,384]{2,0,1:T(4,128)}, f32[3,768,1536]{2,0,1:T(4,128)}, f32[3,768,1536]{2,0,1:T(4,128)}) async-done(((f32[3,768,384]{2,0,1:T(4,128)}, f32[3,768,1536]{2,0,1:T(4,128)}, f32[3,768,1536]{2,0,1:T(4,128)}), (f32[3,768,384]{2,0,1:T(4,128)}, f32[3,768,1536]{2,0,1:T(4,128)}, f32[3,768,1536]{2,0,1:T(4,128)})) %all-reduce.8.cloned.1.call-update) | async-done | bytes 31850512
  1359.2 55.4 %reduce-scatter.14.cloned.1.call-done = f32[48,384]{1,0:T(8,128)} async-done(((f32[768,384]{1,0:T(8,128)}), f32[48,384]{1,0:T(8,128)}) %reduce-scatter.14.cloned.1.call-update) | async-done | bytes 73744 | tf_op jit(solution)/shard_map/reduce_scatter | solution.py:273
  (236 shorter events, 82.0 us)
Async XLA Ops:
  7.2 109.3 %copy-start = (f32[3,1536]{1,0:T(4,128)S(1)}, f32[3,1536]{1,0:T(4,128)}, u32[]{:S(2)}) copy-start(f32[3,1536]{1,0:T(4,128)} %param.28) | copy-start | bytes 55300
  7.2 6.9 copy-start.50
  7.2 7.0 copy-start.47
  7.2 7.0 copy-start.33
  7.2 47.3 %copy-start.48 = (f32[768]{0:T(1024)S(1)}, f32[768]{0:T(1024)}, u32[]{:S(2)}) copy-start(f32[768]{0:T(1024)} %param.20) | copy-start | bytes 9220
  7.2 47.3 %copy-start.39 = (f32[768]{0:T(1024)S(1)}, f32[768]{0:T(1024)}, u32[]{:S(2)}) copy-start(f32[768]{0:T(1024)} %param.19) | copy-start | bytes 9220
  7.2 47.2 %all-gather.8.cloned.1.call-start = ((), (), s32[]{:S(2)}) async-start(), calls=%async_computation.5 | async-start | bytes 1880064 | tf_op jit(solution)/shard_map/all_gather | solution.py:90
  8.0 94.1 %reduce-scatter.16.cloned.1.call-start = ((), (), s32[]{:S(2)}) async-start(), calls=%async_computation.13 | async-start | bytes 2064384
  9.6 48.4 %copy-start.6 = (f32[783,768]{1,0:T(8,128)}, f32[783,768]{1,0:T(8,128)S(1)}, u32[]{:S(2)}) copy-start(f32[783,768]{1,0:T(8,128)S(1)} %reshape.320) | copy-start | bytes 7216132
  12.1 42.4 %copy-start.35 = (f32[783]{0:T(1024)}, f32[783]{0:T(1024)S(1)}, u32[]{:S(2)}) copy-start(f32[783]{0:T(1024)S(1)} %div.55) | copy-start | bytes 9400
  14.0 40.5 %copy-start.37 = (f32[783]{0:T(1024)}, f32[783]{0:T(1024)S(1)}, u32[]{:S(2)}) copy-start(f32[783]{0:T(1024)S(1)} %rsqrt.20) | copy-start | bytes 9400
  76.8 27.5 %copy-start.23 = (bf16[783,384]{0,1:T(8,128)(2,1)}, bf16[783,384]{0,1:T(8,128)(2,1)S(1)}, u32[]{:S(2)}) copy-start(bf16[783,384]{0,1:T(8,128)(2,1)S(1)} %convert_element_type.123) | copy-start | bytes 1804036
  77.6 27.9 %copy-start.44 = (s32[3,261]{1,0:T(4,128)S(1)}, s32[3,261]{1,0:T(4,128)}, u32[]{:S(2)}) copy-start(s32[3,261]{1,0:T(4,128)} %param.18) | copy-start | bytes 9400
  79.2 48.2 %all-gather.10.cloned.1.call-start = ((), (), s32[]{:S(2)}) async-start(), calls=%async_computation.6 | async-start | bytes 1806336 | tf_op jit(solution)/shard_map/all_gather | solution.py:122
  102.1 25.4 %copy-start.46 = (f32[768]{0:T(1024)S(1)}, f32[768]{0:T(1024)}, u32[]{:S(2)}) copy-start(f32[768]{0:T(1024)} %param.24) | copy-start | bytes 9220
  104.3 91.4 %all-gather.12.cloned.1.call-start = ((), (), s32[]{:S(2)}) async-start(), calls=%async_computation.7 | async-start | bytes 7520256 | tf_op jit(solution)/shard_map/all_gather | solution.py:137
  104.8 157.8 %all-gather.14.cloned.1.call-start = ((), (), s32[]{:S(2)}) async-start(), calls=%async_computation.8 | async-start | bytes 7520256 | tf_op jit(solution)/shard_map/all_gather | solution.py:138
  105.4 302.3 %reduce-scatter.20.cloned.1.call-start = ((), (), s32[]{:S(2)}) async-start(), calls=%async_computation.15 | async-start | bytes 2064384
  105.6 10.9 copy-start.30
  109.1 7.7 copy-start.12
  116.5 13.4 copy-start.42
  116.7 13.6 copy-start.34
  116.8 13.6 copy-start.45
  129.9 304.6 %copy-start.3 = (f32[783,768]{1,0:T(8,128)}, f32[783,768]{1,0:T(8,128)S(1)}, u32[]{:S(2)}) copy-start(f32[783,768]{1,0:T(8,128)S(1)} %get-tuple-element.87) | copy-start | bytes 7216132
  294.9 12.2 copy-start.5
  307.0 5.2 copy-start.18
  312.3 14.1 copy-start.19
  364.8 67.0 %all-gather.18.cloned.1.call-start = ((), (), s32[]{:S(2)}) async-start(), calls=%async_computation.10 | async-start | bytes 1806336 | tf_op jit(solution)/shard_map/all_gather | solution.py:211
  410.0 133.4 %reduce-scatter.18.cloned.1.call-start = ((), (), s32[]{:S(2)}) async-start(), calls=%async_computation.14 | async-start | bytes 2064384
  430.8 135.8 %reduce-scatter.22.cloned.1.call-start = ((), (), s32[]{:S(2)}) async-start(), calls=%async_computation.16 | async-start | bytes 2064384
  440.4 5.3 copy-start.26
  447.9 9.1 slice-start
  450.2 6.8 slice-start.1
  457.0 4.4 copy-start.17
  469.8 4.7 copy-start.22
  476.2 69.3 %copy-start.20 = (bf16[1280,768]{1,0:T(8,128)(2,1)S(1)}, bf16[1280,768]{1,0:T(8,128)(2,1)}, u32[]{:S(2)}) copy-start(bf16[1280,768]{1,0:T(8,128)(2,1)} %scatter_custom_fusion.1) | copy-start | bytes 5898244
  476.2 175.0 %all-gather.16.cloned.1.call-start = ((), (), s32[]{:S(2)}) async-start(), calls=%async_computation.9 | async-start | bytes 1806336 | tf_op jit(solution)/shard_map/all_gather | solution.py:159
  545.5 117.8 %all-gather.20.cloned.1.call-start = ((), (), s32[]{:S(2)}) async-start(), calls=%async_computation.11 | async-start | bytes 1806336 | tf_op jit(solution)/shard_map/all_gather | solution.py:265
  568.8 67.1 %copy-start.7 = (f32[783,768]{1,0:T(8,128)S(1)}, f32[783,768]{1,0:T(8,128)}, u32[]{:S(2)}) copy-start(f32[783,768]{1,0:T(8,128)} %copy-done.6) | copy-start | bytes 7216132
  568.8 67.1 %copy-start.36 = (f32[783]{0:T(1024)S(1)}, f32[783]{0:T(1024)}, u32[]{:S(2)}) copy-start(f32[783]{0:T(1024)} %copy-done.35) | copy-start | bytes 9400
  568.8 67.1 %copy-start.38 = (f32[783]{0:T(1024)S(1)}, f32[783]{0:T(1024)}, u32[]{:S(2)}) copy-start(f32[783]{0:T(1024)} %copy-done.37) | copy-start | bytes 9400
  568.8 67.1 %copy-start.40 = (f32[768]{0:T(1024)S(1)}, f32[768]{0:T(1024)}, u32[]{:S(2)}) copy-start(f32[768]{0:T(1024)} %param.19) | copy-start | bytes 9220
  568.8 67.1 %copy-start.49 = (f32[768]{0:T(1024)S(1)}, f32[768]{0:T(1024)}, u32[]{:S(2)}) copy-start(f32[768]{0:T(1024)} %param.20) | copy-start | bytes 9220
  568.9 783.3 %all-reduce.8.cloned.1.call-start = ((), (), s32[]{:S(2)}) async-start(), calls=%async_computation.17 | async-start | bytes 84934656
  647.7 767.0 %reduce-scatter.14.cloned.1.call-start = ((), (), s32[]{:S(2)}) async-start(), calls=%async_computation.12 | async-start | bytes 1253376 | tf_op jit(solution)/shard_map/reduce_scatter | solution.py:273
  651.3 6.4 copy-start.21
  657.7 5.7 copy-start.8
  1353.9 60.8 %copy-start.1 = (f32[3,1536]{1,0:T(4,128)S(1)}, f32[3,1536]{1,0:T(4,128)}, u32[]{:S(2)}) copy-start(f32[3,1536]{1,0:T(4,128)} %param.28) | copy-start | bytes 55300
  (19 other events, 48.8 us)
Sparse Core Ops, SparseCore 0:
  10.4 44.0 all-gather.7
  79.4 22.6 reduce-scatter.15
  104.4 23.0 all-gather.9
  129.6 66.0 all-gather.11
  197.8 64.8 all-gather.13
  365.0 22.7 reduce-scatter.19
  410.1 21.7 all-gather.17
  434.1 23.9 reduce-scatter.17
  476.4 24.2 reduce-scatter.21
  545.6 23.2 all-gather.15
  570.5 23.0 all-gather.19
  647.8 704.3 all-reduce.7
  1356.3 58.2 reduce-scatter.13
where the time goes:
time: 1430 us; the launch traced here: 1420 us
  waiting for transfers between devices  812 us (57%)
  matrix products  278 us (19%)
  local copies, waits for them, and re-layouts  171 us (12%)
  blocking collectives  92.3 us (6%)
  other arithmetic  52.2 us (4%)
  between operations  16 us (1%)
    unnamed x18, waiting for transfers between devices  640 us
    unnamed x128, local copies, waits for them, and re-layouts  67.2 us
    dot_general x1, matrix products, per_device(): jnp.einsum('te,tdf->edf', owner_hot, up_projection_terms, precision=HIGHEST)  67 us
    dot_general x1, matrix products, per_device(): jnp.einsum('te,tdf->edf', owner_hot, down_terms, precision=HIGHEST)  67 us
    psum x1, blocking collectives, per_device(): lax.psum((grad_b_qv, grad_b_out, grad_b_up, grad_b_down, norm_local), 'dp')  65.2 us
    all_gather x1, waiting for transfers between devices, per_device(): lax.all_gather(w_up, 'dp', axis=1, tiled=True)  57.4 us
    reduce_scatter x1, waiting for transfers between devices, per_device(): lax.psum_scatter(grad_out_local, 'dp', scatter_dimension=0, tiled=True)  55.4 us
    all_gather x1, waiting for transfers between devices, per_device(): lax.all_gather(w_down, 'dp', axis=1, tiled=True)  34.1 us
  transfers between devices with their start and end apart: 13, of which 8 were waited for; matrix products, arithmetic and copies ran while one was open for 26% of the time, Pallas kernels for 0%

commit v1 on v0

--- a/solution.py
+++ b/solution.py
@@ -11,6 +11,19 @@
 ROOT_HALF = 0.7071067811865476
 INV_ROOT_TAU = 0.3989422804014327
 HIGHEST = lax.Precision.HIGHEST
+
+
+def collect(value, axis, dim):
+    count, position, rows = (lax.axis_size(axis), lax.axis_index(axis), value.shape[dim])
+    upward = [(i, (i + 1) % count) for i in range(count)]
+    out = jnp.zeros((*value.shape[:dim], count * rows, *value.shape[dim + 1 :]), value.dtype)
+    block = value
+    for hop in range(count):
+        owner = (position - hop) % count
+        out = lax.dynamic_update_slice_in_dim(out, block, owner * rows, axis=dim)
+        if hop < count - 1:
+            block = lax.ppermute(block, axis, upward)
+    return out
 
 
 def norm_rows(vector, gain_vec, shift_vec):
@@ -133,10 +146,7 @@
         .set(second_low)
         .reshape(tile_count, TILE, model_width)
     )
-    up_full, down_full = (
-        lax.all_gather(w_up, "dp", axis=1, tiled=True),
-        lax.all_gather(w_down, "dp", axis=1, tiled=True),
-    )
+    up_full, down_full = (lax.all_gather(w_up, "dp", axis=1, tiled=True), collect(w_down, "dp", 1))
     owner_hot = (tile_owner[:, None] == jnp.arange(expert_count, dtype=jnp.int32)[None, :]).astype(
         jnp.float32
     )

time: 1430 us -> 1530 us (1.070)
  waiting for transfers between devices: 812 us -> 902 us
    ppermute x0 -> x15, waiting for transfers between devices: none -> 196 us  [collect(): block = lax.ppermute(block, axis, upward)]
    all_gather x1, waiting for transfers between devices: 57.4 us -> 0.02 us  [per_device(): lax.all_gather(w_up, 'dp', axis=1, tiled=True)]
    all_gather x1, waiting for transfers between devices: 34.1 us -> 0.01 us  [per_device(): lax.all_gather(w_down, 'dp', axis=1, tiled=True)]
    gather x0 -> x3, local copies, waits for them, and re-layouts: none -> 22.3 us  [per_device(): down_gradient_tiles = down_back[tile_owner]]
    unnamed x128 -> x116, local copies, waits for them, and re-layouts: 67.2 us -> 49.9 us
  transfers between devices with their start and end apart: 13 -> 28, of which waited for: 8 -> 19; matrix products, arithmetic and copies ran while one was open for 26% -> 26% of each run, Pallas kernels for 0% -> 0%
where the time goes in v1:
time: 1530 us
  waiting for transfers between devices  902 us (59%)
  matrix products  281 us (18%)
  local copies, waits for them, and re-layouts  181 us (12%)
  blocking collectives  91.6 us (6%)
  other arithmetic  55.2 us (4%)
  between operations  16.3 us (1%)
    unnamed x18, waiting for transfers between devices  639 us
    ppermute x15, waiting for transfers between devices, collect(): block = lax.ppermute(block, axis, upward)  196 us
    dot_general x1, matrix products, per_device(): jnp.einsum('te,tdf->edf', owner_hot, down_terms, precision=HIGHEST)  66.9 us
    dot_general x1, matrix products, per_device(): jnp.einsum('te,tdf->edf', owner_hot, up_projection_terms, precision=HIGHEST)  66.8 us
    psum x1, blocking collectives, per_device(): lax.psum((grad_b_qv, grad_b_out, grad_b_up, grad_b_down, norm_local), 'dp')  64.8 us
    reduce_scatter x1, waiting for transfers between devices, per_device(): lax.psum_scatter(grad_out_local, 'dp', scatter_dimension=0, tiled=True)  55.4 us
    unnamed x116, local copies, waits for them, and re-layouts  49.9 us
  transfers between devices with their start and end apart: 28, of which 19 were waited for; matrix products, arithmetic and copies ran while one was open for 26% of the time, Pallas kernels for 0%

profile of v1, /device:TPU:0, one launch (start us, length us, event | category | flops | bytes accessed | tf_op | source)
XLA Modules:
  0.0 1527.8 jit_solution(11013524337678914541)
XLA Ops:
  15.6 26.8 %all_gather.28 = bf16[768,384]{1,0:T(8,128)(2,1)} all-gather(bf16[48,384]{1,0:T(8,128)(2,1)} %param.23), channel_id=1, replica_groups=mesh['dp'=16,'rep'=2] {'dp'}, dimensions={0}, use_global_device_ids=true | all-gather | bytes 626688 | tf_op jit(solution)/shard_map/all_gather | solution.py:104
  42.4 12.3 all-gather.8.cloned.1.call-done
  80.4 22.8 %reduce-scatter.16.cloned.1.call-done = bf16[384,783]{1,0:T(8,128)(2,1)} async-done(((bf16[768,783]{1,0:T(8,128)(2,1)}), bf16[384,783]{1,0:T(8,128)(2,1)}) %reduce-scatter.16.cloned.1.call-update) | async-done | bytes 601360
  106.7 10.4 collective-permute-done
  117.3 10.2 collective-permute-done.1
  127.6 10.4 collective-permute-done.2
  139.5 16.6 %collective-permute-done.3 = bf16[3,48,1536]{2,1,0:T(8,128)(2,1)S(1)} collective-permute-done((bf16[3,48,1536]{2,1,0:T(8,128)(2,1)S(1)}, bf16[3,48,1536]{2,1,0:T(8,128)(2,1)S(1)}, u32[]{:S(2)}, u32[]{:S(2)}) %collective-permute-start.3) | collective-permute-done | bytes 442400 | tf_op jit(solution)/shard_map/ppermute | solution.py:25
  158.2 7.4 scatter_custom_fusion.1
  167.5 18.7 %collective-permute-done.5 = bf16[3,48,1536]{2,1,0:T(8,128)(2,1)S(1)} collective-permute-done((bf16[3,48,1536]{2,1,0:T(8,128)(2,1)}, bf16[3,48,1536]{2,1,0:T(8,128)(2,1)S(1)}, u32[]{:S(2)}, u32[]{:S(2)}) %collective-permute-start.5) | collective-permute-done | bytes 442400 | tf_op jit(solution)/shard_map/ppermute | solution.py:25
  186.8 15.7 %collective-permute-done.6 = bf16[3,48,1536]{2,1,0:T(8,128)(2,1)S(1)} collective-permute-done((bf16[3,48,1536]{2,1,0:T(8,128)(2,1)S(1)}, bf16[3,48,1536]{2,1,0:T(8,128)(2,1)S(1)}, u32[]{:S(2)}, u32[]{:S(2)}) %collective-permute-start.6) | collective-permute-done | bytes 442400 | tf_op jit(solution)/shard_map/ppermute | solution.py:25
  202.8 13.3 collective-permute-done.7
  216.2 10.3 collective-permute-done.8
  227.7 18.9 %collective-permute-done.9 = bf16[3,48,1536]{2,1,0:T(8,128)(2,1)S(1)} collective-permute-done((bf16[3,48,1536]{2,1,0:T(8,128)(2,1)S(1)}, bf16[3,48,1536]{2,1,0:T(8,128)(2,1)S(1)}, u32[]{:S(2)}, u32[]{:S(2)}) %collective-permute-start.9) | collective-permute-done | bytes 442400 | tf_op jit(solution)/shard_map/ppermute | solution.py:25
  246.7 10.6 collective-permute-done.10
  258.0 19.4 %collective-permute-done.11 = bf16[3,48,1536]{2,1,0:T(8,128)(2,1)S(1)} collective-permute-done((bf16[3,48,1536]{2,1,0:T(8,128)(2,1)S(1)}, bf16[3,48,1536]{2,1,0:T(8,128)(2,1)S(1)}, u32[]{:S(2)}, u32[]{:S(2)}) %collective-permute-start.11) | collective-permute-done | bytes 442400 | tf_op jit(solution)/shard_map/ppermute | solution.py:25
  277.4 18.9 %collective-permute-done.12 = bf16[3,48,1536]{2,1,0:T(8,128)(2,1)S(1)} collective-permute-done((bf16[3,48,1536]{2,1,0:T(8,128)(2,1)S(1)}, bf16[3,48,1536]{2,1,0:T(8,128)(2,1)S(1)}, u32[]{:S(2)}, u32[]{:S(2)}) %collective-permute-start.12) | collective-permute-done | bytes 442400 | tf_op jit(solution)/shard_map/ppermute | solution.py:25
  296.4 10.3 collective-permute-done.13
  306.9 10.3 collective-permute-done.14
  320.8 7.8 gather_fusion.5
  328.6 7.9 gather_fusion.4
  339.5 8.0 scatter_custom_fusion
  347.5 6.5 fusion.109
  354.0 7.8 gather_fusion.2
  361.8 7.8 gather_fusion.3
  369.7 10.2 constant_dynamic-update-slice_fusion.1
  379.9 6.5 fusion.107
  386.4 7.8 gather_fusion.7
  394.2 8.0 gather_fusion.6
  402.2 10.3 constant_dynamic-update-slice_fusion
  412.5 12.9 fusion.32
  425.4 20.1 %convert_reduce_fusion = (f32[10,1536]{1,0:T(8,128)}, bf16[10,128,1536]{2,1,0:T(8,128)(2,1)}) fusion(f32[10,128,1536]{2,1,0:T(8,128)} %get-tuple-element.101, f32[10,1536]{1,0:T(8,128)S(1)} %fusion.83, bf16[10,128,768]{2,1,0:T(8,128)(2,1)} %bitcast.103, bf16[10,768,768]{2,1,0:T(8,128)(2,1)} %gather_fusion.7, bf16[10,768,768]{2,1,0:T(8,128)(2,1)} %gather_fusion.6), kind=kOutput, calls=%fused_computation.38 | convolution fusion | flops 3092628480 | bytes 37478400 | tf_op jit(solution)/shard_map/pim,pmj->pij/dot_general | solution.py:194
  445.6 14.0 fusion.112
  459.5 6.6 gather_fusion.1
  468.7 20.0 %fusion.14 = bf16[10,128,1536]{2,1,0:T(8,128)(2,1)} fusion(f32[10,128,1536]{2,1,0:T(8,128)} %get-tuple-element.101, f32[10,1536]{1,0:T(8,128)S(1)} %fusion.83, u16[128,1536]{1,0:T(8,128)(2,1)S(1)} %get-tuple-element.67, u16[128,1536]{1,0:T(8,128)(2,1)S(1)} %get-tuple-element.66), kind=kLoop, calls=%fused_computation.26 | loop fusion | flops 139591680 | bytes 12644352 | tf_op jit(solution)/shard_map/convert_element_type | solution.py:161
  488.7 14.2 fusion.4
  503.0 6.6 gather_fusion
  514.2 20.6 %fusion.113 = f32[10,768,1536]{2,1,0:T(8,128)} fusion(bf16[10,128,768]{2,1,0:T(8,128)(2,1)} %bitcast.101, bf16[10,128,1536]{2,1,0:T(8,128)(2,1)} %get-tuple-element.105), kind=kOutput, calls=%fused_computation.219 | convolution fusion | flops 3019898880 | bytes 53084160 | tf_op jit(solution)/shard_map/jxa,jxm->jam/dot_general | solution.py:208
  545.2 4.9 fusion.60
  557.4 6.7 multiply_reduce_fusion
  583.9 66.8 %fusion.2 = f32[3,768,1536]{2,0,1:T(4,128)} fusion(f32[10,768,1536]{2,1,0:T(8,128)} %fusion.113, s32[10]{0:T(128)S(1)} %copy-done.41), kind=kOutput, calls=%fused_computation.12 | convolution fusion | flops 424673312 | bytes 61341736 | tf_op jit(solution)/shard_map/te,tdf->edf/dot_general | solution.py:211
  652.9 20.9 %fusion.114 = f32[10,768,1536]{2,1,0:T(8,128)} fusion(bf16[10,128,768]{2,1,0:T(8,128)(2,1)S(1)} %bitcast.104, bf16[10,128,1536]{2,1,0:T(8,128)(2,1)} %fusion.14), kind=kOutput, calls=%fused_computation.220 | convolution fusion | flops 3019898880 | bytes 53084160 | tf_op jit(solution)/shard_map/jxa,jxm->jam/dot_general | solution.py:204
  676.1 66.9 %fusion = f32[3,768,1536]{2,0,1:T(4,128)} fusion(f32[10,768,1536]{2,1,0:T(8,128)} %fusion.114, s32[10]{0:T(128)S(1)} %copy-done.41), kind=kOutput, calls=%fused_computation.10 | convolution fusion | flops 424673312 | bytes 61341736 | tf_op jit(solution)/shard_map/te,tdf->edf/dot_general | solution.py:207
  743.1 5.4 convolution_bitcast_fusion
  748.5 6.3 copy.153
  766.4 3.9 fusion.96
  779.9 64.8 %all-reduce.4 = (f32[2,384]{1,0:T(2,128)}, f32[768]{0:T(1024)}, f32[3,1536]{1,0:T(4,128)}, f32[3,768]{1,0:T(4,128)}, f32[4,768]{1,0:T(4,128)}) all-reduce(f32[2,384]{1,0:T(2,128)S(1)} %pad_maximum_fusion.5, f32[768]{0:T(1024)S(1)} %get-tuple-element.84, f32[3,1536]{1,0:T(4,128)S(1)} %fusion.81, ...), channel_id=1, replica_groups=mesh['dp'=16,'rep'=2] {'dp'}, use_global_device_ids=true, to_apply=%region_29.30 | all-reduce | flops 11520 | bytes 92160 | tf_op jit(solution)/shard_map/psum | solution.py:286
  844.7 614.0 %all-reduce.8.cloned.1.call-done = (f32[3,768,384]{2,0,1:T(4,128)}, f32[3,768,1536]{2,0,1:T(4,128)}, f32[3,768,1536]{2,0,1:T(4,128)}) async-done(((f32[3,768,384]{2,0,1:T(4,128)}, f32[3,768,1536]{2,0,1:T(4,128)}, f32[3,768,1536]{2,0,1:T(4,128)}), (f32[3,768,384]{2,0,1:T(4,128)}, f32[3,768,1536]{2,0,1:T(4,128)}, f32[3,768,1536]{2,0,1:T(4,128)})) %all-reduce.8.cloned.1.call-update) | async-done | bytes 31850512
  1465.7 55.4 %reduce-scatter.14.cloned.1.call-done = f32[48,384]{1,0:T(8,128)} async-done(((f32[768,384]{1,0:T(8,128)}), f32[48,384]{1,0:T(8,128)}) %reduce-scatter.14.cloned.1.call-update) | async-done | bytes 73744 | tf_op jit(solution)/shard_map/reduce_scatter | solution.py:283
  (274 shorter events, 128.5 us)
Async XLA Ops:
  7.2 195.4 %copy-start = (f32[3,1536]{1,0:T(4,128)S(1)}, f32[3,1536]{1,0:T(4,128)}, u32[]{:S(2)}) copy-start(f32[3,1536]{1,0:T(4,128)} %param.28) | copy-start | bytes 55300
  7.2 47.4 %all-gather.8.cloned.1.call-start = ((), (), s32[]{:S(2)}) async-start(), calls=%async_computation.5 | async-start | bytes 1880064 | tf_op jit(solution)/shard_map/all_gather | solution.py:103
  7.9 95.3 %reduce-scatter.16.cloned.1.call-start = ((), (), s32[]{:S(2)}) async-start(), calls=%async_computation.13 | async-start | bytes 2064384
  9.5 48.6 %copy-start.5 = (f32[783,768]{1,0:T(8,128)}, f32[783,768]{1,0:T(8,128)S(1)}, u32[]{:S(2)}) copy-start(f32[783,768]{1,0:T(8,128)S(1)} %reshape.320) | copy-start | bytes 7216132
  12.0 42.6 %copy-start.34 = (f32[783]{0:T(1024)}, f32[783]{0:T(1024)S(1)}, u32[]{:S(2)}) copy-start(f32[783]{0:T(1024)S(1)} %div.55) | copy-start | bytes 9400
  13.9 40.7 %copy-start.36 = (f32[783]{0:T(1024)}, f32[783]{0:T(1024)S(1)}, u32[]{:S(2)}) copy-start(f32[783]{0:T(1024)S(1)} %rsqrt.20) | copy-start | bytes 9400
  14.8 59.4 %copy-start.28 = (pred[3,261]{1,0:T(4,128)(4,1)}, pred[3,261]{1,0:T(4,128)(4,1)S(1)}, u32[]{:S(2)}) copy-start(pred[3,261]{1,0:T(4,128)(4,1)S(1)} %iota_compare_fusion.4) | copy-start | bytes 2353
  76.4 30.2 %copy-start.24 = (bf16[3,48,1536]{2,1,0:T(8,128)(2,1)S(1)}, bf16[3,48,1536]{2,1,0:T(8,128)(2,1)}, u32[]{:S(2)}) copy-start(bf16[3,48,1536]{2,1,0:T(8,128)(2,1)} %param.29) | copy-start | bytes 1327108
  76.4 40.7 %copy-start.42 = (s32[3,261]{1,0:T(4,128)S(1)}, s32[3,261]{1,0:T(4,128)}, u32[]{:S(2)}) copy-start(s32[3,261]{1,0:T(4,128)} %param.18) | copy-start | bytes 9400
  77.9 78.5 %copy-start.19 = (bf16[783,384]{0,1:T(8,128)(2,1)}, bf16[783,384]{0,1:T(8,128)(2,1)S(1)}, u32[]{:S(2)}) copy-start(bf16[783,384]{0,1:T(8,128)(2,1)S(1)} %convert_element_type.123) | copy-start | bytes 1804036
  80.3 256.2 %all-gather.10.cloned.1.call-start = ((), (), s32[]{:S(2)}) async-start(), calls=%async_computation.6 | async-start | bytes 1806336 | tf_op jit(solution)/shard_map/all_gather | solution.py:135
  105.4 242.1 %all-gather.12.cloned.1.call-start = ((), (), s32[]{:S(2)}) async-start(), calls=%async_computation.7 | async-start | bytes 7520256 | tf_op jit(solution)/shard_map/all_gather | solution.py:149
  106.0 273.9 %all-gather.16.cloned.1.call-start = ((), (), s32[]{:S(2)}) async-start(), calls=%async_computation.9 | async-start | bytes 7520256 | tf_op jit(solution)/shard_map/all_gather | solution.py:182
  106.6 405.4 %reduce-scatter.20.cloned.1.call-start = ((), (), s32[]{:S(2)}) async-start(), calls=%async_computation.15 | async-start | bytes 2064384
  106.6 10.5 collective-permute-start
  117.1 10.4 collective-permute-start.1
  117.2 85.4 %copy-start.30 = (s32[783]{0:T(1024)}, s32[783]{0:T(1024)S(1)}, u32[]{:S(2)}) copy-start(s32[783]{0:T(1024)S(1)} %eq.59) | copy-start | bytes 9400
  127.5 10.4 collective-permute-start.2
  138.0 18.1 %collective-permute-start.3 = (bf16[3,48,1536]{2,1,0:T(8,128)(2,1)S(1)}, bf16[3,48,1536]{2,1,0:T(8,128)(2,1)S(1)}, u32[]{:S(2)}, u32[]{:S(2)}) collective-permute-start(bf16[3,48,1536]{2,1,0:T(8,128)(2,1)S(1)} %collective-permute-done.2), channel_id=1, source_target_pairs={{0,2},{2,4},{4,6},{6,8},{8,10},{10,12},{12,14},{14,16},{16,18},{18... | collective-permute-start | bytes 1327112 | tf_op jit(solution)/shard_map/ppermute | solution.py:25
  156.1 11.4 collective-permute-start.4
  158.0 69.7 %copy-start.10 = (bf16[783,768]{1,0:T(8,128)(2,1)}, bf16[783,768]{1,0:T(8,128)(2,1)S(1)}, u32[]{:S(2)}) copy-start(bf16[783,768]{1,0:T(8,128)(2,1)S(1)} %reshape.398) | copy-start | bytes 3608068
  165.7 50.5 %copy-start.26 = (bf16[3,48,1536]{2,1,0:T(8,128)(2,1)S(1)}, bf16[3,48,1536]{2,1,0:T(8,128)(2,1)}, u32[]{:S(2)}) copy-start(bf16[3,48,1536]{2,1,0:T(8,128)(2,1)} %copy-done.25) | copy-start | bytes 1327108
  167.5 18.8 %collective-permute-start.5 = (bf16[3,48,1536]{2,1,0:T(8,128)(2,1)}, bf16[3,48,1536]{2,1,0:T(8,128)(2,1)S(1)}, u32[]{:S(2)}, u32[]{:S(2)}) collective-permute-start(bf16[3,48,1536]{2,1,0:T(8,128)(2,1)} %collective-permute-done.4), channel_id=1, source_target_pairs={{0,2},{2,4},{4,6},{6,8},{8,10},{10,12},{12,14},{14,16},{16,18},{18... | collective-permute-start | bytes 1327112 | tf_op jit(solution)/shard_map/ppermute | solution.py:25
  186.2 16.3 %collective-permute-start.6 = (bf16[3,48,1536]{2,1,0:T(8,128)(2,1)S(1)}, bf16[3,48,1536]{2,1,0:T(8,128)(2,1)S(1)}, u32[]{:S(2)}, u32[]{:S(2)}) collective-permute-start(bf16[3,48,1536]{2,1,0:T(8,128)(2,1)S(1)} %collective-permute-done.5), channel_id=1, source_target_pairs={{0,2},{2,4},{4,6},{6,8},{8,10},{10,12},{12,14},{14,16},{16,18},{18... | collective-permute-start | bytes 1327112 | tf_op jit(solution)/shard_map/ppermute | solution.py:25
  186.2 60.5 %copy-start.40 = (s32[10]{0:T(128)}, s32[10]{0:T(128)S(1)}, u32[]{:S(2)}) copy-start(s32[10]{0:T(128)S(1)} %broadcast_minimum_fusion) | copy-start | bytes 124
  202.5 13.6 collective-permute-start.7
  216.2 10.4 collective-permute-start.8
  226.6 20.0 %collective-permute-start.9 = (bf16[3,48,1536]{2,1,0:T(8,128)(2,1)S(1)}, bf16[3,48,1536]{2,1,0:T(8,128)(2,1)S(1)}, u32[]{:S(2)}, u32[]{:S(2)}) collective-permute-start(bf16[3,48,1536]{2,1,0:T(8,128)(2,1)S(1)} %collective-permute-done.8), channel_id=1, source_target_pairs={{0,2},{2,4},{4,6},{6,8},{8,10},{10,12},{12,14},{14,16},{16,18},{18... | collective-permute-start | bytes 1327112 | tf_op jit(solution)/shard_map/ppermute | solution.py:25
  246.6 10.7 collective-permute-start.10
  257.3 20.0 %collective-permute-start.11 = (bf16[3,48,1536]{2,1,0:T(8,128)(2,1)S(1)}, bf16[3,48,1536]{2,1,0:T(8,128)(2,1)S(1)}, u32[]{:S(2)}, u32[]{:S(2)}) collective-permute-start(bf16[3,48,1536]{2,1,0:T(8,128)(2,1)S(1)} %collective-permute-done.10), channel_id=1, source_target_pairs={{0,2},{2,4},{4,6},{6,8},{8,10},{10,12},{12,14},{14,16},{16,18},{18... | collective-permute-start | bytes 1327112 | tf_op jit(solution)/shard_map/ppermute | solution.py:25
  277.3 19.0 %collective-permute-start.12 = (bf16[3,48,1536]{2,1,0:T(8,128)(2,1)S(1)}, bf16[3,48,1536]{2,1,0:T(8,128)(2,1)S(1)}, u32[]{:S(2)}, u32[]{:S(2)}) collective-permute-start(bf16[3,48,1536]{2,1,0:T(8,128)(2,1)S(1)} %collective-permute-done.11), channel_id=1, source_target_pairs={{0,2},{2,4},{4,6},{6,8},{8,10},{10,12},{12,14},{14,16},{16,18},{18... | collective-permute-start | bytes 1327112 | tf_op jit(solution)/shard_map/ppermute | solution.py:25
  296.4 10.4 collective-permute-start.13
  306.8 10.4 collective-permute-start.14
  339.0 198.6 %copy-start.3 = (f32[783,768]{1,0:T(8,128)}, f32[783,768]{1,0:T(8,128)S(1)}, u32[]{:S(2)}) copy-start(f32[783,768]{1,0:T(8,128)S(1)} %get-tuple-element.87) | copy-start | bytes 7216132
  468.6 66.4 %all-gather.18.cloned.1.call-start = ((), (), s32[]{:S(2)}) async-start(), calls=%async_computation.10 | async-start | bytes 1806336 | tf_op jit(solution)/shard_map/all_gather | solution.py:221
  514.2 136.5 %reduce-scatter.18.cloned.1.call-start = ((), (), s32[]{:S(2)}) async-start(), calls=%async_computation.14 | async-start | bytes 2064384
  534.8 138.9 %reduce-scatter.22.cloned.1.call-start = ((), (), s32[]{:S(2)}) async-start(), calls=%async_computation.16 | async-start | bytes 2064384
  583.8 69.1 %copy-start.16 = (bf16[1280,768]{1,0:T(8,128)(2,1)S(1)}, bf16[1280,768]{1,0:T(8,128)(2,1)}, u32[]{:S(2)}) copy-start(bf16[1280,768]{1,0:T(8,128)(2,1)} %scatter_custom_fusion.1) | copy-start | bytes 5898244
  583.8 174.6 %all-gather.14.cloned.1.call-start = ((), (), s32[]{:S(2)}) async-start(), calls=%async_computation.8 | async-start | bytes 1806336 | tf_op jit(solution)/shard_map/all_gather | solution.py:169
  652.8 117.5 %all-gather.20.cloned.1.call-start = ((), (), s32[]{:S(2)}) async-start(), calls=%async_computation.11 | async-start | bytes 1806336 | tf_op jit(solution)/shard_map/all_gather | solution.py:275
  676.0 67.1 %copy-start.6 = (f32[783,768]{1,0:T(8,128)S(1)}, f32[783,768]{1,0:T(8,128)}, u32[]{:S(2)}) copy-start(f32[783,768]{1,0:T(8,128)} %copy-done.5) | copy-start | bytes 7216132
  676.0 67.1 %copy-start.35 = (f32[783]{0:T(1024)S(1)}, f32[783]{0:T(1024)}, u32[]{:S(2)}) copy-start(f32[783]{0:T(1024)} %copy-done.34) | copy-start | bytes 9400
  676.0 67.1 %copy-start.37 = (f32[783]{0:T(1024)S(1)}, f32[783]{0:T(1024)}, u32[]{:S(2)}) copy-start(f32[783]{0:T(1024)} %copy-done.36) | copy-start | bytes 9400
  676.0 67.1 %copy-start.38 = (f32[768]{0:T(1024)S(1)}, f32[768]{0:T(1024)}, u32[]{:S(2)}) copy-start(f32[768]{0:T(1024)} %param.19) | copy-start | bytes 9220
  676.0 67.1 %copy-start.45 = (f32[768]{0:T(1024)S(1)}, f32[768]{0:T(1024)}, u32[]{:S(2)}) copy-start(f32[768]{0:T(1024)} %param.20) | copy-start | bytes 9220
  676.1 782.6 %all-reduce.8.cloned.1.call-start = ((), (), s32[]{:S(2)}) async-start(), calls=%async_computation.17 | async-start | bytes 84934656
  754.8 766.2 %reduce-scatter.14.cloned.1.call-start = ((), (), s32[]{:S(2)}) async-start(), calls=%async_computation.12 | async-start | bytes 1253376 | tf_op jit(solution)/shard_map/reduce_scatter | solution.py:283
  772.9 748.1 %copy-start.1 = (f32[3,1536]{1,0:T(4,128)S(1)}, f32[3,1536]{1,0:T(4,128)}, u32[]{:S(2)}) copy-start(f32[3,1536]{1,0:T(4,128)} %param.28) | copy-start | bytes 55300
  (29 other events, 162.0 us)
Sparse Core Ops, SparseCore 0:
  10.3 44.2 all-gather.7
  80.5 22.7 reduce-scatter.15
  105.5 23.0 all-gather.9
  130.7 79.6 all-gather.11
  212.6 81.4 all-gather.15
  468.8 21.2 reduce-scatter.19
  514.3 20.1 all-gather.17
  536.8 23.9 reduce-scatter.17
  583.9 23.4 reduce-scatter.21
  653.0 22.4 all-gather.13
  677.0 23.0 all-gather.19
  754.9 703.6 all-reduce.7
  1462.9 58.1 reduce-scatter.13
